TPU v7x, 32 devices: a whole 2x2x4 slice. The times are simulated.
32 devices in a mesh: field: 2 (over core), dom: 16 (over z, y, x).
Axes of the slice: x: 2, y: 2, z: 4, core: 2. Of those that a mesh axis runs over, the one named last changes fastest.
Arguments:
- modes: float32 [2, 40, 131072], P('field', None, 'dom'), may hold values from -6 to 6
- previous: float32 [2, 40, 131072], P('field', None, 'dom'), may hold values from -6 to 6
- kinds: int32 [2, 3, 256], P('field'), may hold values from 0 to 3
- scales: float32 [2, 3, 256], P('field'), may hold values from 0.5 to 4
- tables: bfloat16 [2, 3, 4, 512, 512], P('field'), may hold values from -2 to 6, as said below
- wet_rows: int32 [2, 49152], P('field', 'dom'), may hold values from 0 to 8191, as said below
- wet_counts: int32 [16], P('dom'), may hold values from 768 to 3072, as said below
- coupling: float32 [49152], P('dom'), may hold values from -6 to 6
Outputs:
- basis: float32 [2, 120, 131072], P('field', None, 'dom')
- projected: float32 [120, 120], replicated
Inputs may be any that keep to these rules, and one draw needn't show every extreme that they name: `tables`: tables of offset 0 are symmetric. `wet_rows`: within each subdomain and field the 3072 row numbers are distinct. `wet_counts`: some subdomain uses all 3072 slots.
All inputs are finite; a program needn't handle non-finite values.
Results may differ from a plain program's by a relative error of at most 0.00045.
The roundings to bfloat16 on the way count: a program that leaves them out, or rounds other values in their place, can miss the bound.
Values may be sent and summed in bfloat16 or wider, within the bound.
A program may use at most 192 MiB of HBM per device.

v0:
```python
import jax
import jax.numpy as jnp
from jax import lax
from jax.sharding import PartitionSpec as P

BS = 512
NTYPE = 4
NBR = 16
IFACE = 3072


def for_sending(shard):
    return jax.tree.map(lambda a: a.astype(jnp.bfloat16) if a.dtype == jnp.float32 else a, shard)


def swapped(shard, axis, apart):
    return lax.ppermute(shard, axis, [(i, i ^ 1 << apart) for i in range(lax.axis_size(axis))])


def extended(cells, sides, width):
    for axis, dim in sides:
        count = lax.axis_size(axis)
        ends = count - 1
        head = lax.slice_in_dim(cells, 0, width, axis=dim)
        tail = lax.slice_in_dim(cells, cells.shape[dim] - width, cells.shape[dim], axis=dim)
        cells = jnp.concatenate(
            [
                lax.ppermute(tail, axis, [(i, (i + 1) % count) for i in range(ends)]),
                cells,
                lax.ppermute(head, axis, [((i + 1) % count, i) for i in range(ends)]),
            ],
            axis=dim,
        )
    return cells


def typed_product(blocks, table_set, type_ids, factors, transposed):
    columns = blocks.shape[0]
    count = blocks.shape[1]
    flattened = blocks.reshape(columns * count, BS)
    contract = 0 if transposed else 1
    result = jnp.zeros((columns, count, BS), jnp.float32)
    for type_id in range(NTYPE):
        product = lax.dot_general(
            flattened,
            table_set[type_id],
            (((1,), (contract,)), ((), ())),
            preferred_element_type=jnp.float32,
        )
        factor_t = jnp.where(type_ids == type_id, factors, jnp.float32(0.0))
        result = result + factor_t[None, :, None] * product.reshape(columns, count, BS)
    return result


def block_product(window, kinds, scales, tables):
    columns = window.shape[0]
    blocks = window.reshape(columns, NBR + 4, BS)
    result = typed_product(blocks[:, 2 : NBR + 2], tables[0], kinds[0, 2:], scales[0, 2:], False)
    for offset in (1, 2):
        result = result + typed_product(
            blocks[:, 2 + offset : NBR + 2 + offset],
            tables[offset],
            kinds[offset, 2:],
            scales[offset, 2:],
            False,
        )
        result = result + typed_product(
            blocks[:, 2 - offset : NBR + 2 - offset],
            tables[offset],
            kinds[offset, 2 - offset : NBR + 2 - offset],
            scales[offset, 2 - offset : NBR + 2 - offset],
            True,
        )
    return result.reshape(columns, NBR * BS)


def operate(window, vectors, kinds, scales, tables, rows, weights):
    images = block_product(window, kinds, scales, tables)
    values = jnp.take(vectors, rows, axis=1) * weights[None, :]
    received = swapped(for_sending(values), "field", 0).astype(values.dtype)
    return images.at[:, rows].add(received)


def shards(modes, previous, kinds, scales, tables, wet_rows, wet_counts, coupling):
    highest = lax.Precision.HIGHEST
    domain = lax.axis_index("dom")
    vec_modes = modes[0]
    vec_prev = previous[0]
    field_tables = tables[0]
    kinds_pad = jnp.pad(kinds[0], ((0, 0), (2, 0)))
    scales_pad = jnp.pad(scales[0], ((0, 0), (2, 0)))
    local_kinds = lax.dynamic_slice_in_dim(kinds_pad, domain * NBR, NBR + 2, 1)
    local_scales = lax.dynamic_slice_in_dim(scales_pad, domain * NBR, NBR + 2, 1)
    rows = wet_rows[0]
    used = jnp.arange(IFACE, dtype=jnp.int32) < wet_counts[0]
    weights = jnp.where(used, coupling, jnp.float32(0.0))
    window_modes = extended(vec_modes.astype(jnp.bfloat16), (("dom", 1),), 2 * BS)
    image_x = operate(
        window_modes, vec_modes, local_kinds, local_scales, field_tables, rows, weights
    )
    squares, products = lax.psum(
        (jnp.sum(vec_modes * vec_modes, axis=1), jnp.sum(vec_modes * image_x, axis=1)),
        ("field", "dom"),
    )
    quotient = products / squares
    diag_table = jnp.diagonal(field_tables[0], axis1=1, axis2=2).astype(jnp.float32)
    selector = (local_kinds[0, 2:][:, None] == jnp.arange(NTYPE, dtype=jnp.int32)[None, :]).astype(
        jnp.float32
    )
    row_diag = jnp.dot(selector, diag_table, precision=highest)
    jacobi = (local_scales[0, 2:][:, None] * row_diag).reshape(NBR * BS)
    residual_dir = (image_x - vec_modes * quotient[:, None]) / jacobi[None, :]
    pair = jnp.concatenate([residual_dir, vec_prev], axis=0)
    window_pair = extended(pair.astype(jnp.bfloat16), (("dom", 1),), 2 * BS)
    image_wp = operate(window_pair, pair, local_kinds, local_scales, field_tables, rows, weights)
    search = jnp.concatenate([vec_modes, pair], axis=0)
    image_all = jnp.concatenate([image_x, image_wp], axis=0)
    ndof = 2.0 * lax.axis_size("dom") * NBR * BS
    summed_b, summed_a = lax.psum(
        (
            jnp.dot(search, search.T, precision=highest),
            jnp.dot(search, image_all.T, precision=highest),
        ),
        ("field", "dom"),
    )
    gram_b = summed_b / ndof
    gram_a = (summed_a + summed_a.T) / (2.0 * ndof)
    chol = jnp.linalg.cholesky(gram_b)
    leading = jax.scipy.linalg.solve_triangular(chol, gram_a, lower=True)
    projected = jax.scipy.linalg.solve_triangular(chol, leading.T, lower=True)
    basis = jax.scipy.linalg.solve_triangular(chol, search, lower=True)
    return (basis[None], projected)


def solution(mesh):
    return jax.shard_map(
        shards,
        mesh=mesh,
        in_specs=(
            P("field", None, "dom"),
            P("field", None, "dom"),
            P("field", None, None),
            P("field", None, None),
            P("field", None, None, None, None),
            P("field", "dom"),
            P("dom"),
            P("dom"),
        ),
        out_specs=(P("field", None, "dom"), P()),
        check_vma=False,
    )
```

profile of v0, /device:TPU:0, one launch (start us, length us, event | category | flops | bytes accessed | tf_op | source)
XLA Modules:
  0.0 542.5 jit_solution(1693732785863256557)
XLA Ops:
  7.2 3.7 copy.30
  14.2 5.6 %collective-permute-start = (bf16[40,1024]{0,1:T(8,128)(2,1)}, bf16[40,1024]{0,1:T(8,128)(2,1)}, u32[]{:S(2)}, u32[]{:S(2)}) collective-permute-start(bf16[40,1024]{0,1:T(8,128)(2,1)} %get-tuple-element.18), channel_id=1, source_target_pairs={{0,1},{1,2},{2,3},{3,4},{4,5},{5,6},{6,7},{7,8},{8,9},{9,10},{10,1... | collective-permute-start | bytes 245768 | tf_op jit(solution)/shard_map/ppermute | solution.py:28
  21.7 13.1 %gather_fusion = f32[3072,40]{1,0:T(8,128)} fusion(f32[40,8192]{0,1:T(8,128)} %bitcast.254, s32[3072]{0:T(1024)S(1)} %broadcast_clamp_fusion), kind=kCustom, calls=%fused_computation | custom fusion | bytes 995328 | tf_op jit(solution)/shard_map/jit(_take)/gather | solution.py:79
  41.7 41.6 %copy.52 = bf16[1,1,4,512,512]{2,4,3,1,0:T(8,128)(2,1)} copy(bf16[1,1,4,512,512]{4,3,2,1,0:T(8,128)(2,1)S(1)} %slice-done.8) | data formatting | bytes 4194304
  83.3 6.5 %gather_fusion.1 = bf16[512,4]{1,0:T(8,128)(2,1)S(1)} fusion(bf16[4,512,512]{0,2,1:T(8,128)(2,1)} %bitcast.58, s32[512]{0:T(512)S(1)} %bitcast.269), kind=kCustom, calls=%fused_computation.1 | custom fusion | bytes 12288 | tf_op jit(solution)/shard_map/jit(diagonal)/gather | solution.py:106
  90.0 3.9 copy.38
  116.3 19.6 %scatter_fusion = f32[40,8192]{0,1:T(8,128)} fusion(f32[40,8192]{0,1:T(8,128)} %bitcast.256, s32[3072]{0:T(1024)S(1)} %bitcast.271, f32[3072,40]{1,0:T(8,128)S(1)} %copy.36), kind=kCustom, calls=%fused_computation.3 | custom fusion | flops 122880 | bytes 1486848 | tf_op jit(solution)/shard_map/scatter-add | solution.py:81
  135.9 4.6 multiply_reduce_fusion
  140.4 41.7 %all-reduce.3 = (f32[40]{0:T(128)S(1)}, f32[40]{0:T(128)S(1)}) all-reduce(f32[40]{0:T(128)S(1)} %get-tuple-element.4, f32[40]{0:T(128)S(1)} %get-tuple-element.3), channel_id=1, replica_groups=mesh['field'=2,'dom'=16] {'field','dom'}, use_global_device_ids=true, to_apply=%region_2.3 | all-reduce | flops 80 | bytes 640 | tf_op jit(solution)/shard_map/psum | solution.py:101
  182.2 6.0 %subtract_divide_fusion = f32[40,8192]{0,1:T(8,128)S(1)} fusion(f32[40,8192]{0,1:T(8,128)} %scatter_fusion, f32[8192]{0:T(1024)S(1)} %bitcast.273, f32[40]{0:T(128)S(1)} %div.33, f32[1,40,8192]{1,2,0:T(8,128)} %copy.30), kind=kLoop, calls=%fused_computation.12 | loop fusion | flops 983040 | bytes 3965088 | tf_op jit(solution)/shard_map/div | solution.py:112
  191.3 4.2 pad_maximum_fusion
  196.4 4.2 collective-permute-start.3
  201.9 13.5 %gather_fusion.2 = f32[3072,80]{1,0:T(8,128)} fusion(f32[80,8192]{0,1:T(8,128)} %get-tuple-element.10, s32[3072]{0:T(1024)S(1)} %broadcast_clamp_fusion), kind=kCustom, calls=%fused_computation.2 | custom fusion | bytes 1978368 | tf_op jit(solution)/shard_map/jit(_take)/gather | solution.py:79
  219.3 10.8 %fusion.178 = f32[120,120]{0,1:T(8,128)} fusion(f32[120,8192]{0,1:T(8,128)} %pad_maximum_fusion), kind=kOutput, calls=%fused_computation.259 | convolution fusion | flops 1415577600 | bytes 3989760 | tf_op jit(solution)/shard_map/dot_general | solution.py:121
  230.1 7.7 %pad_maximum_fusion.2 = bf16[80,10240]{0,1:T(8,128)(2,1)S(1)} fusion(bf16[80,1024]{0,1:T(8,128)(2,1)S(1)} %collective-permute-done.4, bf16[80,8192]{0,1:T(8,128)(2,1)S(1)} %get-tuple-element.9, bf16[80,1024]{0,1:T(8,128)(2,1)S(1)} %collective-permute-done.3), kind=kLoop, calls=%fused_computation.15 | loop fusion | flops 4915200 | bytes 3276800 | tf_op jit(solution)/shard_map/concatenate | solution.py:26
  237.8 4.2 fusion.175
  245.3 3.6 fusion.26
  260.0 3.8 fusion.39
  263.8 3.6 fusion.45
  270.5 3.5 fusion.43
  292.1 3.9 fusion.67
  296.0 4.4 copy.54
  300.5 4.0 fusion.63
  304.5 4.0 fusion.69
  317.9 19.0 %add_add_fusion = f32[80,16,512]{2,1,0:T(8,128)} fusion(f32[80,16,512]{2,1,0:T(8,128)} %fusion.43, f32[80,16,512]{2,1,0:T(8,128)} %fusion.49, f32[80,16,512]{2,1,0:T(8,128)} %fusion.55, f32[80,16,512]{2,1,0:T(8,128)} %fusion.39, f32[80,16,512]{2,1,0:T(8,128)} %fusion.45, f32[80,16,512]{2,1,0:T(8,128)} %fusion.51, f32[80,16,512]{2,1,0:T(8,128)} %fusion.57, ...), kind=kOutput, calls=%fused_computation.16 | convolution fusion | flops 696647680 | bytes 54265088 | tf_op jit(solution)/shard_map/dot_general | solution.py:44
  336.9 4.9 copy.49
  343.4 19.6 %scatter_fusion.1 = f32[80,8192]{0,1:T(8,128)} fusion(f32[80,8192]{0,1:T(8,128)} %bitcast.258, s32[3072]{0:T(1024)S(1)} %bitcast.272, f32[3072,80]{1,0:T(8,128)S(1)} %copy.44), kind=kCustom, calls=%fused_computation.4 | custom fusion | flops 245760 | bytes 2961408 | tf_op jit(solution)/shard_map/scatter-add | solution.py:81
  363.0 13.1 %fusion = f32[120,120]{1,0:T(8,128)} fusion(f32[120,8192]{0,1:T(8,128)} %pad_maximum_fusion, f32[80,8192]{0,1:T(8,128)} %scatter_fusion.1, f32[40,8192]{0,1:T(8,128)} %scatter_fusion), kind=kOutput, calls=%fused_computation.8 | convolution fusion | flops 1416560640 | bytes 7921920 | tf_op jit(solution)/shard_map/dot_general | solution.py:122
  376.2 125.3 %all-reduce.6.cloned.1.call-done = (f32[120,120]{0,1:T(8,128)}, f32[120,120]{1,0:T(8,128)}) async-done(((f32[120,120]{0,1:T(8,128)}, f32[120,120]{1,0:T(8,128)}), (f32[120,120]{0,1:T(8,128)}, f32[120,120]{1,0:T(8,128)})) %all-reduce.6.cloned.1.call-update) | async-done | bytes 115216 | tf_op jit(solution)/shard_map/psum | solution.py:119
  503.3 11.0 %cholesky.16 = f32[120,120]{1,0:T(8,128)S(1)} custom-call(f32[120,120]{1,0:T(8,128)S(1)} %fusion.152), custom_call_target="Cholesky" | custom-call | tf_op jit(solution)/shard_map/jit(cholesky)/cholesky | solution.py:128
  515.6 9.5 %custom-call.10 = f32[1,120,120]{1,2,0:T(8,128)S(1)} custom-call(f32[1,120,120]{2,1,0:T(8,128)S(1)} %fusion.145), custom_call_target="InvertDiagBlocksLowerTriangular" | custom-call | tf_op jit(solution)/shard_map/jit(_solve_triangular)/triangular_solve | solution.py:131
  526.0 7.9 %convolution_bitcast_fusion = f32[1,120,8192]{2,1,0:T(8,128)} fusion(f32[120,8192]{0,1:T(8,128)} %pad_maximum_fusion, f32[1,120,120]{1,2,0:T(8,128)S(1)} %custom-call.10), kind=kOutput, calls=%fused_computation.5 | convolution fusion | flops 1415577600 | bytes 7921920 | tf_op jit(solution)/shard_map/jit(_solve_triangular)/triangular_solve | solution.py:131
  (139 shorter events, 94.8 us)
Async XLA Ops:
  7.2 494.4 %all-reduce.6.cloned.1.call-start = ((), (), s32[]{:S(2)}) async-start(), calls=%async_computation | async-start | bytes 245760 | tf_op jit(solution)/shard_map/psum | solution.py:119
  10.9 10.1 %copy-start.9 = (s32[1,3072]{1,0:T(1,128)S(1)}, s32[1,3072]{1,0:T(1,128)}, u32[]{:S(2)}) copy-start(s32[1,3072]{1,0:T(1,128)} %param.15) | copy-start | bytes 36868
  13.3 21.5 %copy-start.10 = (f32[3072]{0:T(1024)S(1)}, f32[3072]{0:T(1024)}, u32[]{:S(2)}) copy-start(f32[3072]{0:T(1024)} %param.17) | copy-start | bytes 36868
  14.2 79.7 %collective-permute-start = (bf16[40,1024]{0,1:T(8,128)(2,1)}, bf16[40,1024]{0,1:T(8,128)(2,1)}, u32[]{:S(2)}, u32[]{:S(2)}) collective-permute-start(bf16[40,1024]{0,1:T(8,128)(2,1)} %get-tuple-element.18), channel_id=1, source_target_pairs={{0,1},{1,2},{2,3},{3,4},{4,5},{5,6},{6,7},{7,8},{8,9},{9,10},{10,1... | collective-permute-start | bytes 245768 | tf_op jit(solution)/shard_map/ppermute | solution.py:28
  19.7 75.2 %collective-permute-start.1 = (bf16[40,1024]{0,1:T(8,128)(2,1)}, bf16[40,1024]{0,1:T(8,128)(2,1)S(1)}, u32[]{:S(2)}, u32[]{:S(2)}) collective-permute-start(bf16[40,1024]{0,1:T(8,128)(2,1)} %get-tuple-element.19), channel_id=1, source_target_pairs={{1,0},{2,1},{3,2},{4,3},{5,4},{6,5},{7,6},{8,7},{9,8},{10,9},{11,1... | collective-permute-start | bytes 245768 | tf_op jit(solution)/shard_map/ppermute | solution.py:30
  34.8 5.3 copy-start.11
  34.8 5.3 copy-start.12
  38.6 76.2 %collective-permute-start.2 = (bf16[40,3072]{1,0:T(8,128)(2,1)}, bf16[40,3072]{1,0:T(8,128)(2,1)}, u32[]{:S(2)}, u32[]{:S(2)}) collective-permute-start(bf16[40,3072]{1,0:T(8,128)(2,1)} %copy.34), channel_id=1, source_target_pairs={{0,16},{16,0},{1,17},{17,1},{2,18},{18,2},{3,19},{19,3},{4,20},{20... | collective-permute-start | bytes 737288 | tf_op jit(solution)/shard_map/ppermute | solution.py:17
  40.1 1.6 slice-start.8
  90.0 5.1 copy-start.7
  95.7 8.2 %slice-start = ((s8[6291456]{0:T(1024)(128)(4,1)}), s8[4194304]{0:T(1024)(128)(4,1)S(1)}, s32[]{:S(2)}) async-start(s8[6291456]{0:T(1024)(128)(4,1)} %bitcast.259), calls=%async_computation.1 | async-start | bytes 8388608
  99.0 4.9 slice-start.1
  182.1 6.0 %copy-start.1 = (f32[1,40,8192]{1,2,0:T(8,128)S(1)}, f32[1,40,8192]{1,2,0:T(8,128)}, u32[]{:S(2)}) copy-start(f32[1,40,8192]{1,2,0:T(8,128)} %copy.38) | copy-start | bytes 3932164
  188.2 3.2 copy-start
  196.4 33.7 %collective-permute-start.3 = (bf16[80,1024]{0,1:T(8,128)(2,1)}, bf16[80,1024]{0,1:T(8,128)(2,1)S(1)}, u32[]{:S(2)}, u32[]{:S(2)}) collective-permute-start(bf16[80,1024]{0,1:T(8,128)(2,1)} %get-tuple-element.16), channel_id=1, source_target_pairs={{0,1},{1,2},{2,3},{3,4},{4,5},{5,6},{6,7},{7,8},{8,9},{9,10},{10,1... | collective-permute-start | bytes 491528 | tf_op jit(solution)/shard_map/ppermute | solution.py:28
  200.6 29.5 %collective-permute-start.4 = (bf16[80,1024]{0,1:T(8,128)(2,1)}, bf16[80,1024]{0,1:T(8,128)(2,1)S(1)}, u32[]{:S(2)}, u32[]{:S(2)}) collective-permute-start(bf16[80,1024]{0,1:T(8,128)(2,1)} %get-tuple-element.17), channel_id=1, source_target_pairs={{1,0},{2,1},{3,2},{4,3},{5,4},{6,5},{7,6},{8,7},{9,8},{10,9},{11,1... | collective-permute-start | bytes 491528 | tf_op jit(solution)/shard_map/ppermute | solution.py:30
  219.3 122.5 %collective-permute-start.5 = (bf16[80,3072]{1,0:T(8,128)(2,1)}, bf16[80,3072]{1,0:T(8,128)(2,1)}, u32[]{:S(2)}, u32[]{:S(2)}) collective-permute-start(bf16[80,3072]{1,0:T(8,128)(2,1)} %copy.42), channel_id=1, source_target_pairs={{0,16},{16,0},{1,17},{17,1},{2,18},{18,2},{3,19},{19,3},{4,20},{20... | collective-permute-start | bytes 1474568 | tf_op jit(solution)/shard_map/ppermute | solution.py:17
  242.0 10.2 %slice-start.2 = ((s8[6291456]{0:T(1024)(128)(4,1)}), s8[2097152]{0:T(1024)(128)(4,1)S(1)}, s32[]{:S(2)}) async-start(s8[6291456]{0:T(1024)(128)(4,1)} %bitcast.261), calls=%async_computation.3 | async-start | bytes 4194304
  245.2 7.0 %slice-start.3 = ((s8[6291456]{0:T(1024)(128)(4,1)}), s8[4194304]{0:T(1024)(128)(4,1)S(1)}, s32[]{:S(2)}) async-start(s8[6291456]{0:T(1024)(128)(4,1)} %bitcast.261), calls=%async_computation.4 | async-start | bytes 8388608
  260.0 7.4 %copy-start.4 = (bf16[80,16,512]{2,1,0:T(8,128)(2,1)}, bf16[80,16,512]{2,1,0:T(8,128)(2,1)S(1)}, u32[]{:S(2)}) copy-start(bf16[80,16,512]{2,1,0:T(8,128)(2,1)S(1)} %copy.56) | copy-start | bytes 3932164
  263.8 13.7 %slice-start.4 = ((s8[6291456]{0:T(1024)(128)(4,1)}), s8[2097152]{0:T(1024)(128)(4,1)S(1)}, s32[]{:S(2)}) async-start(s8[6291456]{0:T(1024)(128)(4,1)} %bitcast.263), calls=%async_computation.5 | async-start | bytes 4194304
  270.5 7.0 %slice-start.5 = ((s8[6291456]{0:T(1024)(128)(4,1)}), s8[4194304]{0:T(1024)(128)(4,1)S(1)}, s32[]{:S(2)}) async-start(s8[6291456]{0:T(1024)(128)(4,1)} %bitcast.263), calls=%async_computation.6 | async-start | bytes 8388608
  274.0 3.5 copy-start.5
  287.7 1.1 copy-start.2
  292.1 16.3 %slice-start.6 = ((s8[6291456]{0:T(1024)(128)(4,1)}), s8[2097152]{0:T(1024)(128)(4,1)S(1)}, s32[]{:S(2)}) async-start(s8[6291456]{0:T(1024)(128)(4,1)} %bitcast.265), calls=%async_computation.7 | async-start | bytes 4194304
  300.5 8.0 %slice-start.7 = ((s8[6291456]{0:T(1024)(128)(4,1)}), s8[4194304]{0:T(1024)(128)(4,1)S(1)}, s32[]{:S(2)}) async-start(s8[6291456]{0:T(1024)(128)(4,1)} %bitcast.265), calls=%async_computation.8 | async-start | bytes 8388608
  304.5 4.0 copy-start.3
  308.4 2.3 copy-start.6
  526.0 7.9 %copy-start.8 = (f32[120,120]{1,0:T(8,128)S(1)}, f32[120,120]{1,0:T(8,128)}, u32[]{:S(2)}) copy-start(f32[120,120]{1,0:T(8,128)} %get-tuple-element.6) | copy-start | bytes 172804
Sparse Core Ops, SparseCore 0:
  376.3 125.1 all-reduce.5
where the time goes:
time: 547 us; the launch traced here: 543 us
  matrix products  126 us (23%)
  waiting for transfers between devices  125 us (23%)
  local copies, waits for them, and re-layouts  122 us (22%)
  other arithmetic  98.6 us (18%)
  blocking collectives  41.7 us (8%)
  between operations  15.8 us (3%)
  starting transfers between devices  12.4 us (2%)
    psum x1, waiting for transfers between devices, shards(): lax.psum((jnp.dot(search, search.T, precision=highest), jnp.dot(search, i...  125 us
    dot_general x40, matrix products, typed_product(): lax.dot_general(flattened, table_set[type_id], (((1,), (contract,)), ((),...  93 us
    unnamed x53, local copies, waits for them, and re-layouts  67.2 us
    psum x1, blocking collectives, shards(): lax.psum((jnp.sum(vec_modes * vec_modes, axis=1), jnp.sum(vec_modes * ima...  41.7 us
    scatter-add x2, other arithmetic, operate(): return images.at[:, rows].add(received)  39.2 us
    gather x2, local copies, waits for them, and re-layouts, operate(): values = jnp.take(vectors, rows, axis=1) * weights[None, :]  26.6 us
    dot_general x1, matrix products, shards(): jnp.dot(search, image_all.T, precision=highest)  13.1 us
    another operation x3, other arithmetic, shards(): chol = jnp.linalg.cholesky(gram_b)  11.6 us
  transfers between devices with their start and end apart: 7, of which 1 were waited for; matrix products, arithmetic and copies ran while one was open for 42% of the time, Pallas kernels for 0%

commit v1 on v0

--- a/solution.py
+++ b/solution.py
@@ -117,11 +117,14 @@
     image_all = jnp.concatenate([image_x, image_wp], axis=0)
     ndof = 2.0 * lax.axis_size("dom") * NBR * BS
     summed_b, summed_a = lax.psum(
-        (
-            jnp.dot(search, search.T, precision=highest),
-            jnp.dot(search, image_all.T, precision=highest),
+        lax.psum(
+            (
+                jnp.dot(search, search.T, precision=highest),
+                jnp.dot(search, image_all.T, precision=highest),
+            ),
+            "dom",
         ),
-        ("field", "dom"),
+        "field",
     )
     gram_b = summed_b / ndof
     gram_a = (summed_a + summed_a.T) / (2.0 * ndof)

time: 547 us -> 549 us (level)
    psum x0 -> x1, waiting for transfers between devices: none -> 19.4 us  [shards(): lax.psum(lax.psum((jnp.dot(search, search.T, precision=highest), jnp.dot(...]
    psum x1, waiting for transfers between devices: 125 us -> 107 us  [shards(): lax.psum((jnp.dot(search, search.T, precision=highest), jnp.dot(search, i...]
  transfers between devices with their start and end apart: 7 -> 8, of which waited for: 1 -> 2; matrix products, arithmetic and copies ran while one was open for 42% -> 42% of each run, Pallas kernels for 0% -> 0%
where the time goes in v1:
time: 549 us; the launch traced here: 544 us
  matrix products  126 us (23%)
  waiting for transfers between devices  126 us (23%)
  local copies, waits for them, and re-layouts  122 us (22%)
  other arithmetic  98.4 us (18%)
  blocking collectives  41.7 us (8%)
  between operations  15.9 us (3%)
  starting transfers between devices  12.7 us (2%)
    psum x1, waiting for transfers between devices, shards(): lax.psum((jnp.dot(search, search.T, precision=highest), jnp.dot(search, i...  107 us
    dot_general x40, matrix products, typed_product(): lax.dot_general(flattened, table_set[type_id], (((1,), (contract,)), ((),...  93 us
    unnamed x53, local copies, waits for them, and re-layouts  67.2 us
    psum x1, blocking collectives, shards(): lax.psum((jnp.sum(vec_modes * vec_modes, axis=1), jnp.sum(vec_modes * ima...  41.7 us
    scatter-add x2, other arithmetic, operate(): return images.at[:, rows].add(received)  39.2 us
    gather x2, local copies, waits for them, and re-layouts, operate(): values = jnp.take(vectors, rows, axis=1) * weights[None, :]  26.6 us
    psum x1, waiting for transfers between devices, shards(): lax.psum(lax.psum((jnp.dot(search, search.T, precision=highest), jnp.dot(...  19.4 us
    dot_general x1, matrix products, shards(): jnp.dot(search, image_all.T, precision=highest)  13.1 us
  transfers between devices with their start and end apart: 8, of which 2 were waited for; matrix products, arithmetic and copies ran while one was open for 42% of the time, Pallas kernels for 0%

profile of v1, /device:TPU:0, one launch (start us, length us, event | category | flops | bytes accessed | tf_op | source)
XLA Modules:
  0.0 543.7 jit_solution(9636974827668413956)
XLA Ops:
  7.2 3.7 copy.30
  14.2 5.6 %collective-permute-start = (bf16[40,1024]{0,1:T(8,128)(2,1)}, bf16[40,1024]{0,1:T(8,128)(2,1)}, u32[]{:S(2)}, u32[]{:S(2)}) collective-permute-start(bf16[40,1024]{0,1:T(8,128)(2,1)} %get-tuple-element.20), channel_id=1, source_target_pairs={{0,1},{1,2},{2,3},{3,4},{4,5},{5,6},{6,7},{7,8},{8,9},{9,10},{10,1... | collective-permute-start | bytes 245768 | tf_op jit(solution)/shard_map/ppermute | solution.py:28
  21.7 13.1 %gather_fusion = f32[3072,40]{1,0:T(8,128)} fusion(f32[40,8192]{0,1:T(8,128)} %bitcast.254, s32[3072]{0:T(1024)S(1)} %broadcast_clamp_fusion), kind=kCustom, calls=%fused_computation | custom fusion | bytes 995328 | tf_op jit(solution)/shard_map/jit(_take)/gather | solution.py:79
  41.8 41.6 %copy.52 = bf16[1,1,4,512,512]{2,4,3,1,0:T(8,128)(2,1)} copy(bf16[1,1,4,512,512]{4,3,2,1,0:T(8,128)(2,1)S(1)} %slice-done.8) | data formatting | bytes 4194304
  83.3 6.4 %gather_fusion.1 = bf16[512,4]{1,0:T(8,128)(2,1)S(1)} fusion(bf16[4,512,512]{0,2,1:T(8,128)(2,1)} %bitcast.58, s32[512]{0:T(512)S(1)} %bitcast.269), kind=kCustom, calls=%fused_computation.1 | custom fusion | bytes 12288 | tf_op jit(solution)/shard_map/jit(diagonal)/gather | solution.py:106
  90.0 3.9 copy.38
  116.3 19.6 %scatter_fusion = f32[40,8192]{0,1:T(8,128)} fusion(f32[40,8192]{0,1:T(8,128)} %bitcast.256, s32[3072]{0:T(1024)S(1)} %bitcast.271, f32[3072,40]{1,0:T(8,128)S(1)} %copy.36), kind=kCustom, calls=%fused_computation.3 | custom fusion | flops 122880 | bytes 1486848 | tf_op jit(solution)/shard_map/scatter-add | solution.py:81
  135.9 4.6 multiply_reduce_fusion
  140.4 41.7 %all-reduce.2 = (f32[40]{0:T(128)S(1)}, f32[40]{0:T(128)S(1)}) all-reduce(f32[40]{0:T(128)S(1)} %get-tuple-element.4, f32[40]{0:T(128)S(1)} %get-tuple-element.3), channel_id=1, replica_groups=mesh['field'=2,'dom'=16] {'field','dom'}, use_global_device_ids=true, to_apply=%region_2.3 | all-reduce | flops 80 | bytes 640 | tf_op jit(solution)/shard_map/psum | solution.py:101
  182.1 6.0 %subtract_divide_fusion = f32[40,8192]{0,1:T(8,128)S(1)} fusion(f32[40,8192]{0,1:T(8,128)} %scatter_fusion, f32[8192]{0:T(1024)S(1)} %bitcast.273, f32[40]{0:T(128)S(1)} %div.33, f32[1,40,8192]{1,2,0:T(8,128)} %copy.30), kind=kLoop, calls=%fused_computation.12 | loop fusion | flops 983040 | bytes 3965088 | tf_op jit(solution)/shard_map/div | solution.py:112
  191.3 4.2 pad_maximum_fusion
  196.4 4.2 collective-permute-start.3
  201.9 13.5 %gather_fusion.2 = f32[3072,80]{1,0:T(8,128)} fusion(f32[80,8192]{0,1:T(8,128)} %get-tuple-element.12, s32[3072]{0:T(1024)S(1)} %broadcast_clamp_fusion), kind=kCustom, calls=%fused_computation.2 | custom fusion | bytes 1978368 | tf_op jit(solution)/shard_map/jit(_take)/gather | solution.py:79
  219.3 10.8 %fusion.178 = f32[120,120]{0,1:T(8,128)} fusion(f32[120,8192]{0,1:T(8,128)} %pad_maximum_fusion), kind=kOutput, calls=%fused_computation.259 | convolution fusion | flops 1415577600 | bytes 3989760 | tf_op jit(solution)/shard_map/dot_general | solution.py:122
  230.1 7.7 %pad_maximum_fusion.2 = bf16[80,10240]{0,1:T(8,128)(2,1)S(1)} fusion(bf16[80,1024]{0,1:T(8,128)(2,1)S(1)} %collective-permute-done.4, bf16[80,8192]{0,1:T(8,128)(2,1)S(1)} %get-tuple-element.11, bf16[80,1024]{0,1:T(8,128)(2,1)S(1)} %collective-permute-done.3), kind=kLoop, calls=%fused_computation.15 | loop fusion | flops 4915200 | bytes 3276800 | tf_op jit(solution)/shard_map/concatenate | solution.py:26
  237.8 4.2 fusion.175
  245.3 3.6 fusion.26
  260.0 3.8 fusion.39
  263.8 3.6 fusion.45
  292.1 3.9 fusion.67
  296.0 4.4 copy.54
  300.4 4.0 fusion.63
  304.4 4.0 fusion.69
  317.8 19.0 %add_add_fusion = f32[80,16,512]{2,1,0:T(8,128)} fusion(f32[80,16,512]{2,1,0:T(8,128)} %fusion.43, f32[80,16,512]{2,1,0:T(8,128)} %fusion.49, f32[80,16,512]{2,1,0:T(8,128)} %fusion.55, f32[80,16,512]{2,1,0:T(8,128)} %fusion.39, f32[80,16,512]{2,1,0:T(8,128)} %fusion.45, f32[80,16,512]{2,1,0:T(8,128)} %fusion.51, f32[80,16,512]{2,1,0:T(8,128)} %fusion.57, ...), kind=kOutput, calls=%fused_computation.16 | convolution fusion | flops 696647680 | bytes 54265088 | tf_op jit(solution)/shard_map/dot_general | solution.py:44
  336.8 4.9 copy.49
  343.4 19.6 %scatter_fusion.1 = f32[80,8192]{0,1:T(8,128)} fusion(f32[80,8192]{0,1:T(8,128)} %bitcast.258, s32[3072]{0:T(1024)S(1)} %bitcast.272, f32[3072,80]{1,0:T(8,128)S(1)} %copy.44), kind=kCustom, calls=%fused_computation.4 | custom fusion | flops 245760 | bytes 2961408 | tf_op jit(solution)/shard_map/scatter-add | solution.py:81
  363.0 13.1 %fusion = f32[120,120]{1,0:T(8,128)} fusion(f32[120,8192]{0,1:T(8,128)} %pad_maximum_fusion, f32[80,8192]{0,1:T(8,128)} %scatter_fusion.1, f32[40,8192]{0,1:T(8,128)} %scatter_fusion), kind=kOutput, calls=%fused_computation.8 | convolution fusion | flops 1416560640 | bytes 7921920 | tf_op jit(solution)/shard_map/dot_general | solution.py:123
  376.5 107.0 %all-reduce.8.cloned.1.call-done = (f32[120,120]{0,1:T(8,128)}, f32[120,120]{1,0:T(8,128)}) async-done(((f32[120,120]{0,1:T(8,128)}, f32[120,120]{1,0:T(8,128)}), (f32[120,120]{0,1:T(8,128)}, f32[120,120]{1,0:T(8,128)})) %all-reduce.8.cloned.1.call-update) | async-done | bytes 115216 | tf_op jit(solution)/shard_map/psum | solution.py:120
  483.6 19.4 %all-reduce.10.cloned.1.call-done = (f32[120,120]{0,1:T(8,128)}, f32[120,120]{1,0:T(8,128)}) async-done(((f32[120,120]{0,1:T(8,128)}, f32[120,120]{1,0:T(8,128)}), (f32[120,120]{0,1:T(8,128)}, f32[120,120]{1,0:T(8,128)})) %all-reduce.10.cloned.1.call-update) | async-done | bytes 115216 | tf_op jit(solution)/shard_map/psum | solution.py:119
  504.7 11.0 %cholesky.16 = f32[120,120]{1,0:T(8,128)S(1)} custom-call(f32[120,120]{1,0:T(8,128)S(1)} %fusion.152), custom_call_target="Cholesky" | custom-call | tf_op jit(solution)/shard_map/jit(cholesky)/cholesky | solution.py:131
  517.1 9.2 %custom-call.10 = f32[1,120,120]{1,2,0:T(8,128)S(1)} custom-call(f32[1,120,120]{2,1,0:T(8,128)S(1)} %fusion.145), custom_call_target="InvertDiagBlocksLowerTriangular" | custom-call | tf_op jit(solution)/shard_map/jit(_solve_triangular)/triangular_solve | solution.py:134
  527.2 7.9 %convolution_bitcast_fusion = f32[1,120,8192]{2,1,0:T(8,128)} fusion(f32[120,8192]{0,1:T(8,128)} %pad_maximum_fusion, f32[1,120,120]{1,2,0:T(8,128)S(1)} %custom-call.10), kind=kOutput, calls=%fused_computation.5 | convolution fusion | flops 1415577600 | bytes 7921920 | tf_op jit(solution)/shard_map/jit(_solve_triangular)/triangular_solve | solution.py:134
  (142 shorter events, 98.6 us)
Async XLA Ops:
  7.2 476.4 %all-reduce.8.cloned.1.call-start = ((), (), s32[]{:S(2)}) async-start(), calls=%async_computation | async-start | bytes 245760 | tf_op jit(solution)/shard_map/psum | solution.py:120
  10.9 10.1 %copy-start.9 = (s32[1,3072]{1,0:T(1,128)S(1)}, s32[1,3072]{1,0:T(1,128)}, u32[]{:S(2)}) copy-start(s32[1,3072]{1,0:T(1,128)} %param.15) | copy-start | bytes 36868
  13.3 21.5 %copy-start.10 = (f32[3072]{0:T(1024)S(1)}, f32[3072]{0:T(1024)}, u32[]{:S(2)}) copy-start(f32[3072]{0:T(1024)} %param.17) | copy-start | bytes 36868
  14.2 79.7 %collective-permute-start = (bf16[40,1024]{0,1:T(8,128)(2,1)}, bf16[40,1024]{0,1:T(8,128)(2,1)}, u32[]{:S(2)}, u32[]{:S(2)}) collective-permute-start(bf16[40,1024]{0,1:T(8,128)(2,1)} %get-tuple-element.20), channel_id=1, source_target_pairs={{0,1},{1,2},{2,3},{3,4},{4,5},{5,6},{6,7},{7,8},{8,9},{9,10},{10,1... | collective-permute-start | bytes 245768 | tf_op jit(solution)/shard_map/ppermute | solution.py:28
  19.8 75.2 %collective-permute-start.1 = (bf16[40,1024]{0,1:T(8,128)(2,1)}, bf16[40,1024]{0,1:T(8,128)(2,1)S(1)}, u32[]{:S(2)}, u32[]{:S(2)}) collective-permute-start(bf16[40,1024]{0,1:T(8,128)(2,1)} %get-tuple-element.21), channel_id=1, source_target_pairs={{1,0},{2,1},{3,2},{4,3},{5,4},{6,5},{7,6},{8,7},{9,8},{10,9},{11,1... | collective-permute-start | bytes 245768 | tf_op jit(solution)/shard_map/ppermute | solution.py:30
  34.9 5.3 copy-start.11
  34.9 5.3 copy-start.12
  38.7 76.2 %collective-permute-start.2 = (bf16[40,3072]{1,0:T(8,128)(2,1)}, bf16[40,3072]{1,0:T(8,128)(2,1)}, u32[]{:S(2)}, u32[]{:S(2)}) collective-permute-start(bf16[40,3072]{1,0:T(8,128)(2,1)} %copy.34), channel_id=1, source_target_pairs={{0,16},{16,0},{1,17},{17,1},{2,18},{18,2},{3,19},{19,3},{4,20},{20... | collective-permute-start | bytes 737288 | tf_op jit(solution)/shard_map/ppermute | solution.py:17
  40.2 1.6 slice-start.8
  90.0 5.2 copy-start.7
  95.7 8.2 %slice-start = ((s8[6291456]{0:T(1024)(128)(4,1)}), s8[4194304]{0:T(1024)(128)(4,1)S(1)}, s32[]{:S(2)}) async-start(s8[6291456]{0:T(1024)(128)(4,1)} %bitcast.259), calls=%async_computation.2 | async-start | bytes 8388608
  99.1 4.9 slice-start.1
  182.1 6.0 %copy-start.1 = (f32[1,40,8192]{1,2,0:T(8,128)S(1)}, f32[1,40,8192]{1,2,0:T(8,128)}, u32[]{:S(2)}) copy-start(f32[1,40,8192]{1,2,0:T(8,128)} %copy.38) | copy-start | bytes 3932164
  188.2 3.2 copy-start
  196.4 33.7 %collective-permute-start.3 = (bf16[80,1024]{0,1:T(8,128)(2,1)}, bf16[80,1024]{0,1:T(8,128)(2,1)S(1)}, u32[]{:S(2)}, u32[]{:S(2)}) collective-permute-start(bf16[80,1024]{0,1:T(8,128)(2,1)} %get-tuple-element.18), channel_id=1, source_target_pairs={{0,1},{1,2},{2,3},{3,4},{4,5},{5,6},{6,7},{7,8},{8,9},{9,10},{10,1... | collective-permute-start | bytes 491528 | tf_op jit(solution)/shard_map/ppermute | solution.py:28
  200.6 29.5 %collective-permute-start.4 = (bf16[80,1024]{0,1:T(8,128)(2,1)}, bf16[80,1024]{0,1:T(8,128)(2,1)S(1)}, u32[]{:S(2)}, u32[]{:S(2)}) collective-permute-start(bf16[80,1024]{0,1:T(8,128)(2,1)} %get-tuple-element.19), channel_id=1, source_target_pairs={{1,0},{2,1},{3,2},{4,3},{5,4},{6,5},{7,6},{8,7},{9,8},{10,9},{11,1... | collective-permute-start | bytes 491528 | tf_op jit(solution)/shard_map/ppermute | solution.py:30
  219.3 122.5 %collective-permute-start.5 = (bf16[80,3072]{1,0:T(8,128)(2,1)}, bf16[80,3072]{1,0:T(8,128)(2,1)}, u32[]{:S(2)}, u32[]{:S(2)}) collective-permute-start(bf16[80,3072]{1,0:T(8,128)(2,1)} %copy.42), channel_id=1, source_target_pairs={{0,16},{16,0},{1,17},{17,1},{2,18},{18,2},{3,19},{19,3},{4,20},{20... | collective-permute-start | bytes 1474568 | tf_op jit(solution)/shard_map/ppermute | solution.py:17
  242.0 10.2 %slice-start.2 = ((s8[6291456]{0:T(1024)(128)(4,1)}), s8[2097152]{0:T(1024)(128)(4,1)S(1)}, s32[]{:S(2)}) async-start(s8[6291456]{0:T(1024)(128)(4,1)} %bitcast.261), calls=%async_computation.4 | async-start | bytes 4194304
  245.2 7.0 %slice-start.3 = ((s8[6291456]{0:T(1024)(128)(4,1)}), s8[4194304]{0:T(1024)(128)(4,1)S(1)}, s32[]{:S(2)}) async-start(s8[6291456]{0:T(1024)(128)(4,1)} %bitcast.261), calls=%async_computation.5 | async-start | bytes 8388608
  260.0 7.4 %copy-start.4 = (bf16[80,16,512]{2,1,0:T(8,128)(2,1)}, bf16[80,16,512]{2,1,0:T(8,128)(2,1)S(1)}, u32[]{:S(2)}) copy-start(bf16[80,16,512]{2,1,0:T(8,128)(2,1)S(1)} %copy.56) | copy-start | bytes 3932164
  263.8 13.7 %slice-start.4 = ((s8[6291456]{0:T(1024)(128)(4,1)}), s8[2097152]{0:T(1024)(128)(4,1)S(1)}, s32[]{:S(2)}) async-start(s8[6291456]{0:T(1024)(128)(4,1)} %bitcast.263), calls=%async_computation.6 | async-start | bytes 4194304
  270.5 7.0 %slice-start.5 = ((s8[6291456]{0:T(1024)(128)(4,1)}), s8[4194304]{0:T(1024)(128)(4,1)S(1)}, s32[]{:S(2)}) async-start(s8[6291456]{0:T(1024)(128)(4,1)} %bitcast.263), calls=%async_computation.7 | async-start | bytes 8388608
  274.0 3.5 copy-start.5
  287.7 1.1 copy-start.2
  292.1 16.3 %slice-start.6 = ((s8[6291456]{0:T(1024)(128)(4,1)}), s8[2097152]{0:T(1024)(128)(4,1)S(1)}, s32[]{:S(2)}) async-start(s8[6291456]{0:T(1024)(128)(4,1)} %bitcast.265), calls=%async_computation.8 | async-start | bytes 4194304
  300.4 8.0 %slice-start.7 = ((s8[6291456]{0:T(1024)(128)(4,1)}), s8[4194304]{0:T(1024)(128)(4,1)S(1)}, s32[]{:S(2)}) async-start(s8[6291456]{0:T(1024)(128)(4,1)} %bitcast.265), calls=%async_computation.9 | async-start | bytes 8388608
  304.4 4.0 copy-start.3
  308.4 2.3 copy-start.6
  376.2 126.8 %all-reduce.10.cloned.1.call-start = ((), (), s32[]{:S(2)}) async-start(), calls=%async_computation.1 | async-start | bytes 245760 | tf_op jit(solution)/shard_map/psum | solution.py:119
  527.2 7.9 %copy-start.8 = (f32[120,120]{1,0:T(8,128)S(1)}, f32[120,120]{1,0:T(8,128)}, u32[]{:S(2)}) copy-start(f32[120,120]{1,0:T(8,128)} %get-tuple-element.10) | copy-start | bytes 172804
Sparse Core Ops, SparseCore 0:
  376.3 107.1 all-reduce.7
  485.9 16.9 all-reduce.9
